TPU v7x, 512 devices: a 8x2x16 block of a 8x8x16 slice. The times are simulated.
512 devices in a mesh: subj: 2 (over y), row: 16 (over x, core), col: 16 (over z).
Axes of the slice: x: 8, y: 2, z: 16, core: 2. Of those that a mesh axis runs over, the one named last changes fastest.
The devices are a block of a 8x8x16 slice.
Arguments:
- series: float32 [800, 65536], P(None, ('subj', 'row', 'col')), parts along dimension 1, as said below
- keep_mask: int32 [512, 256], P(('subj', 'row'), 'col'), parts along dimension 0, may hold values from 0 to 1, as said below
- row_owner: int32 [512], P('subj'), parts along dimension 0, may hold values from 0 to 15, as said below
Outputs:
- owned_tiles: bfloat16 [32, 16, 96, 128, 128], P(('subj', 'row'), 'col'), parts along dimension 0
- owned_ids: int32 [32, 16, 96], P(('subj', 'row'), 'col'), parts along dimension 0
There are 2 independent parts, one for each index of `subj`. A program takes and returns all parts, laid end to end along the dimension named above; each array names one. Nothing has to cross between parts.
Inputs may be any that keep to these rules, and one draw needn't show every extreme that they name: Each voxel's series varies over time. `keep_mask`: of the 16 tiles that one tile row has in one column block, at most 6 are kept; in every draw one owner keeps exactly 6 in each of its tile rows in some column block. `row_owner`: the 16 tile rows of a row block have 16 different owners, and every owner holds 16 tile rows, from 16 different row blocks.
All inputs are finite; a program needn't handle non-finite values.
Results may differ from a plain program's by a relative error of at most 0.0042.
Values may be sent and summed in bfloat16 or wider, within the bound.
No kernel may reach another device: no remote copies, remote signals or barrier semaphores. Data moves between devices by JAX's collectives and lax.ppermute only.
A program may use at most 64 MiB of HBM per device.

v0:
```python
import jax
import jax.numpy as jnp
from jax import lax
from jax.sharding import PartitionSpec as P

TILE = 128
epsilon = 1e-05


def compact(flat_tiles, flat_ids, capacity):
    is_valid = (flat_ids >= 0).astype(jnp.int32)
    running = jnp.cumsum(is_valid)
    slot_index = jnp.arange(capacity, dtype=jnp.int32)
    position = jnp.arange(flat_ids.shape[0], dtype=jnp.int32)
    slot_hit = (is_valid[None, :] == 1) & (running[None, :] == slot_index[:, None] + 1)
    picked = jnp.sum(jnp.where(slot_hit, position[None, :], 0), axis=1)
    present = running[-1] > slot_index
    chosen = jnp.take(flat_tiles, picked, axis=0)
    slot_tiles = jnp.where(present[:, None, None], chosen, jnp.zeros_like(chosen))
    slot_ids = jnp.where(present, jnp.take(flat_ids, picked), -1).astype(jnp.int32)
    return (slot_tiles, slot_ids)


def shards(series, keep_mask, row_owner):
    frames = series.shape[0]
    average = jnp.mean(series, axis=0, keepdims=True)
    centred = series - average
    spread = jnp.mean(centred * centred, axis=0, keepdims=True)
    scored = (centred * lax.rsqrt(spread + epsilon)).astype(jnp.bfloat16)
    row_block = lax.all_gather(scored, "col", axis=1, tiled=True)
    product = lax.dot_general(
        row_block,
        lax.all_gather(scored, "row", axis=1, tiled=True),
        (((0,), (0,)), ((), ())),
        preferred_element_type=jnp.float32,
    )
    tile_grid = (product * (1.0 / frames)).astype(jnp.bfloat16)
    row_count, col_count = keep_mask.shape
    tile_grid = tile_grid.reshape(row_count, TILE, col_count, TILE).transpose(0, 2, 1, 3)
    row_devices = lax.axis_size("row")
    col_devices = lax.axis_size("col")
    row_index = lax.axis_index("row")
    col_index = lax.axis_index("col")
    total_cols = col_count * col_devices
    slot_limit = max(2, 3 * col_count // 8)
    capacity = row_count * slot_limit
    local_owner = lax.dynamic_slice_in_dim(row_owner, row_index * row_count, row_count)
    targets = jnp.arange(row_devices, dtype=jnp.int32)
    owns_row = local_owner[None, :] == targets[:, None]
    has_row = jnp.any(owns_row, axis=1)
    row_of = jnp.sum(
        jnp.where(owns_row, jnp.arange(row_count, dtype=jnp.int32)[None, :], 0), axis=1
    )
    keep_flags = jnp.where(has_row[:, None], jnp.take(keep_mask, row_of, axis=0), 0)
    global_row = row_index * row_count + row_of
    first_col = col_index * col_count
    running = jnp.cumsum(keep_flags, axis=1)
    slot_index = jnp.arange(slot_limit, dtype=jnp.int32)
    slot_hit = (keep_flags[:, None, :] == 1) & (
        running[:, None, :] == slot_index[None, :, None] + 1
    )
    picked = jnp.sum(
        jnp.where(slot_hit, jnp.arange(col_count, dtype=jnp.int32)[None, None, :], 0), axis=2
    )
    present = running[:, -1:] > slot_index[None, :]
    chosen = tile_grid[row_of[:, None], picked]
    outgoing = jnp.where(present[:, :, None, None], chosen, jnp.zeros_like(chosen))
    out_ids = jnp.where(present, global_row[:, None] * total_cols + first_col + picked, -1)
    incoming, in_ids = (
        lax.all_to_all(outgoing, "row", split_axis=0, concat_axis=0, tiled=True),
        lax.all_to_all(out_ids, "row", split_axis=0, concat_axis=0, tiled=True),
    )
    flat_tiles = incoming.reshape(-1, TILE, TILE)
    flat_ids = in_ids.reshape(-1)
    slot_tiles, slot_ids = compact(flat_tiles, flat_ids, capacity)
    return (slot_tiles.reshape(1, 1, capacity, TILE, TILE), slot_ids.reshape(1, 1, capacity))


def solution(mesh):
    in_specs = (P(None, ("subj", "row", "col")), P(("subj", "row"), "col"), P("subj"))
    out_specs = (P(("subj", "row"), "col", None, None, None), P(("subj", "row"), "col", None))
    return jax.shard_map(shards, mesh=mesh, in_specs=in_specs, out_specs=out_specs, check_vma=False)
```

profile of v0, /device:TPU:65, one launch (start us, length us, event | category | flops | bytes accessed | tf_op | source)
XLA Modules:
  0.0 313.3 jit_solution(12894685114126903149)
XLA Ops:
  7.2 0.0 copy-start
  7.2 0.1 all-gather.3.cloned.1.call-start
  7.3 1.1 reduce_sum.60
  8.4 1.1 multiply_reduce_fusion
  9.5 1.7 multiply_convert_fusion.1
  11.3 0.1 all-gather.3.cloned.1.call-update
  11.3 0.1 all-gather.5.cloned.1.call-start
  11.4 0.7 all-gather.5.cloned.1.call-update
  12.1 0.8 dynamic_slice.3
  12.9 0.1 select_reduce_fusion.2
  13.0 0.0 copy-done
  13.0 0.6 gather_fusion
  13.6 0.1 fusion.3
  13.7 0.1 broadcast_compare_fusion
  13.8 0.2 reduce_window_sum.18
  14.0 0.2 slice_reduce_fusion
  14.2 0.3 select_reduce_fusion.1
  14.4 0.7 copy.18
  15.1 44.6 %all-to-all-start = ((s32[16,1,6]{2,1,0:T(1,128)}), s32[16,1,6]{2,1,0:T(1,128)S(1)}, u32[]{:S(2)}, u32[]{:S(2)}) async-start(s32[16,1,6]{2,1,0:T(1,128)} %copy.18), calls=%async_computation | async-start | bytes 16384 | tf_op jit(solution)/shard_map/all_to_all | solution.py:71
  59.8 0.1 copy.21
  59.9 0.1 reshape.311
  59.9 0.1 iota_compare_fusion
  60.0 64.0 %all-gather.3.cloned.1.call-done = bf16[800,2048]{1,0:T(8,128)(2,1)} async-done(((bf16[800,128]{1,0:T(8,128)(2,1)}), bf16[800,2048]{1,0:T(8,128)(2,1)}) %all-gather.3.cloned.1.call-update) | async-done | bytes 3276816 | tf_op jit(solution)/shard_map/all_gather | solution.py:30
  124.0 61.5 %all-gather.5.cloned.1.call-done = bf16[800,2048]{1,0:T(8,128)(2,1)} async-done(((bf16[800,128]{1,0:T(8,128)(2,1)}), bf16[800,2048]{1,0:T(8,128)(2,1)}) %all-gather.5.cloned.1.call-update) | async-done | bytes 3276816 | tf_op jit(solution)/shard_map/all_gather | solution.py:33
  185.5 13.6 %fusion = bf16[256,8,16,128]{3,1,2,0:T(8,128)(2,1)} fusion(bf16[800,2048]{1,0:T(8,128)(2,1)} %all-gather.3.cloned.1.call-done, bf16[800,2048]{1,0:T(8,128)(2,1)} %all-gather.5.cloned.1.call-done), kind=kOutput, calls=%fused_computation.6 | convolution fusion | flops 6719275008 | bytes 14942208 | tf_op jit(solution)/shard_map/dot_general | solution.py:31
  199.2 9.7 %copy.22 = bf16[256,8,16,128]{3,2,1,0:T(8,128)(2,1)} copy(bf16[256,8,16,128]{3,1,2,0:T(8,128)(2,1)} %fusion) | data formatting | bytes 16777216
  208.9 9.1 %copy.24 = bf16[16,128,16,128]{3,1,2,0:T(8,128)(2,1)} copy(bf16[16,128,16,128]{3,2,1,0:T(8,128)(2,1)} %bitcast.36) | data formatting | bytes 16777216 | tf_op jit(solution)/shard_map/reshape | solution.py:39
  218.0 4.9 %gather_fusion.1 = bf16[96,128,128]{2,1,0:T(8,128)(2,1)S(1)} fusion(bf16[16,16,128,128]{3,2,1,0:T(8,128)(2,1)} %bitcast.37, s32[96]{0:T(128)S(1)} %reshape.311), kind=kCustom, calls=%fused_computation.1 | custom fusion | bytes 6292224 | tf_op jit(solution)/shard_map/gather | solution.py:66
  223.0 1.9 broadcast_select_fusion
  224.9 0.0 all-to-all-done
  224.9 4.5 %all-to-all-start.1 = ((bf16[16,6,128,128]{3,2,1,0:T(8,128)(2,1)}), bf16[16,6,128,128]{3,2,1,0:T(8,128)(2,1)S(1)}, u32[]{:S(2)}, u32[]{:S(2)}) async-start(bf16[16,6,128,128]{3,2,1,0:T(8,128)(2,1)} %broadcast_select_fusion), calls=%async_computation.1 | async-start | bytes 6291456 | tf_op jit(solution)/shard_map/all_to_all | solution.py:70
  229.4 0.5 broadcast.364
  229.9 0.7 fusion.11
  230.6 0.1 reshape.333
  230.7 0.1 reduce-window.4
  230.8 0.1 reduce.3
  230.9 0.6 slice.21
  231.5 0.1 reshape.299
  231.6 0.2 select_reduce_fusion
  231.8 1.2 gather_fusion.3
  233.1 0.7 compare_and_fusion
  233.8 1.2 compare_select_fusion.6
  235.0 65.3 %all-to-all-done.1 = bf16[16,6,128,128]{3,2,1,0:T(8,128)(2,1)S(1)} async-done(((bf16[16,6,128,128]{3,2,1,0:T(8,128)(2,1)}), bf16[16,6,128,128]{3,2,1,0:T(8,128)(2,1)S(1)}, u32[]{:S(2)}, u32[]{:S(2)}) %all-to-all-start.1) | async-done | bytes 3145760 | tf_op jit(solution)/shard_map/all_to_all | solution.py:70
  300.3 2.7 gather_fusion.2
  303.0 3.4 %fusion.1 = bf16[1,1,96,128,128]{4,3,2,1,0:T(8,128)(2,1)} fusion(bf16[96,128,128]{2,1,0:T(8,128)(2,1)} %gather_fusion.2, pred[96]{0:T(512)(128)(4,1)S(1)} %get-tuple-element.8, pred[96]{0:T(512)(128)(4,1)S(1)} %get-tuple-element.9), kind=kLoop, calls=%fused_computation.8 | loop fusion | flops 3145728 | bytes 6291648 | tf_op jit(solution)/shard_map/jit(_where)/select_n | solution.py:19
  (13 shorter events, 0.1 us)
Async XLA Ops:
  7.2 5.9 %copy-start = (s32[16,16]{1,0:T(8,128)S(1)}, s32[16,16]{1,0:T(8,128)}, u32[]{:S(2)}) copy-start(s32[16,16]{1,0:T(8,128)} %param.4) | copy-start | bytes 3076
  7.2 116.8 %all-gather.3.cloned.1.call-start = ((), (), s32[]{:S(2)}) async-start(), calls=%async_computation.2 | async-start | bytes 3481600 | tf_op jit(solution)/shard_map/all_gather | solution.py:30
  11.3 174.2 %all-gather.5.cloned.1.call-start = ((), (), s32[]{:S(2)}) async-start(), calls=%async_computation.3 | async-start | bytes 3481600 | tf_op jit(solution)/shard_map/all_gather | solution.py:33
  15.1 209.8 %all-to-all-start = ((s32[16,1,6]{2,1,0:T(1,128)}), s32[16,1,6]{2,1,0:T(1,128)S(1)}, u32[]{:S(2)}, u32[]{:S(2)}) async-start(s32[16,1,6]{2,1,0:T(1,128)} %copy.18), calls=%async_computation | async-start | bytes 16384 | tf_op jit(solution)/shard_map/all_to_all | solution.py:71
  224.9 75.4 %all-to-all-start.1 = ((bf16[16,6,128,128]{3,2,1,0:T(8,128)(2,1)}), bf16[16,6,128,128]{3,2,1,0:T(8,128)(2,1)S(1)}, u32[]{:S(2)}, u32[]{:S(2)}) async-start(bf16[16,6,128,128]{3,2,1,0:T(8,128)(2,1)} %broadcast_select_fusion), calls=%async_computation.1 | async-start | bytes 6291456 | tf_op jit(solution)/shard_map/all_to_all | solution.py:70
Sparse Core Ops, SparseCore 0:
  11.4 112.5 all-gather.2
  126.6 58.8 all-gather.4
where the time goes:
time: 314 us; the launch traced here: 313 us
  waiting for transfers between devices  192 us (61%)
  starting transfers between devices  49.2 us (16%)
  local copies, waits for them, and re-layouts  31.4 us (10%)
  between operations  14.2 us (5%)
  matrix products  13.6 us (4%)
  other arithmetic  13.2 us (4%)
    all_to_all x1, waiting for transfers between devices, shards(): lax.all_to_all(outgoing, 'row', split_axis=0, concat_axis=0, tiled=True)  65.3 us
    all_gather x1, waiting for transfers between devices, shards(): row_block = lax.all_gather(scored, 'col', axis=1, tiled=True)  64 us
    all_gather x1, waiting for transfers between devices, shards(): lax.all_gather(scored, 'row', axis=1, tiled=True)  61.5 us
    all_to_all x1, starting transfers between devices, shards(): lax.all_to_all(out_ids, 'row', split_axis=0, concat_axis=0, tiled=True)  44.6 us
    dot_general x1, matrix products, shards(): lax.dot_general(row_block, lax.all_gather(scored, 'row', axis=1, tiled=Tr...  13.6 us
    unnamed x3, local copies, waits for them, and re-layouts  9.76 us
    reshape x1, local copies, waits for them, and re-layouts, shards(): tile_grid.reshape(row_count, TILE, col_count, TILE).transpose(0, 2, 1, 3)  9.11 us
  transfers between devices with their start and end apart: 4, of which 3 were waited for; matrix products, arithmetic and copies ran while one was open for 15% of the time, Pallas kernels for 0%

commit v1 on v0

--- a/solution.py
+++ b/solution.py
@@ -27,7 +27,19 @@
     centred = series - average
     spread = jnp.mean(centred * centred, axis=0, keepdims=True)
     scored = (centred * lax.rsqrt(spread + epsilon)).astype(jnp.bfloat16)
-    row_block = lax.all_gather(scored, "col", axis=1, tiled=True)
+    total_devices = lax.axis_size("col")
+    pages = [(k0, (k0 + 1) % total_devices) for k0 in range(total_devices)]
+    all_rows, later = ([scored], [scored])
+    log = [(k0, (k0 - 1) % total_devices) for k0 in range(total_devices)]
+    for _ in range(total_devices // 2):
+        all_rows.append(lax.ppermute(all_rows[-1], "col", perm=pages))
+    for _ in range((total_devices - 1) // 2):
+        later.append(lax.ppermute(later[-1], "col", log))
+    row_block = jnp.roll(
+        jnp.concatenate([*all_rows[::-1], *later[1:]], axis=1),
+        shift=(lax.axis_index("col") - total_devices // 2) * scored.shape[1],
+        axis=1,
+    )
     product = lax.dot_general(
         row_block,
         lax.all_gather(scored, "row", axis=1, tiled=True),

time: 314 us -> 288 us (0.917)
  waiting for transfers between devices: 192 us -> 77.4 us
  starting transfers between devices: 49.2 us -> 113 us
  local copies, waits for them, and re-layouts: 31.4 us -> 53.1 us
    ppermute x0 -> x15, starting transfers between devices: none -> 90.2 us  [the longest x7 70.1 us: shards(): later.append(lax.ppermute(later[-1], 'col', log))]
    all_gather x1 -> x0, waiting for transfers between devices: 64 us -> none  [shards(): row_block = lax.all_gather(scored, 'col', axis=1, tiled=True)]
    all_gather x1, waiting for transfers between devices: 61.5 us -> 0.01 us  [shards(): lax.all_gather(scored, 'row', axis=1, tiled=True)]
    all_to_all x1, starting transfers between devices: 44.6 us -> 14 us  [shards(): lax.all_to_all(out_ids, 'row', split_axis=0, concat_axis=0, tiled=True)]
    unnamed x3 -> x36, local copies, waits for them, and re-layouts: 9.76 us -> 30.8 us
    ppermute x0 -> x15, waiting for transfers between devices: none -> 12 us  [the longest x8 8.86 us: shards(): all_rows.append(lax.ppermute(all_rows[-1], 'col', perm=pages))]
    all_to_all x1, starting transfers between devices: 4.46 us -> 9.11 us  [shards(): lax.all_to_all(outgoing, 'row', split_axis=0, concat_axis=0, tiled=True)]
  transfers between devices with their start and end apart: 4 -> 18, of which waited for: 3 -> 8; matrix products, arithmetic and copies ran while one was open for 15% -> 25% of each run, Pallas kernels for 0% -> 0%
where the time goes in v1:
time: 288 us; the launch traced here: 287 us
  starting transfers between devices  113 us (39%)
  waiting for transfers between devices  77.4 us (27%)
  local copies, waits for them, and re-layouts  53.1 us (18%)
  other arithmetic  15.2 us (5%)
  between operations  14.4 us (5%)
  matrix products  13.6 us (5%)
    ppermute x7, starting transfers between devices, shards(): later.append(lax.ppermute(later[-1], 'col', log))  70.1 us
    all_to_all x1, waiting for transfers between devices, shards(): lax.all_to_all(outgoing, 'row', split_axis=0, concat_axis=0, tiled=True)  65.3 us
    unnamed x36, local copies, waits for them, and re-layouts  30.8 us
    ppermute x8, starting transfers between devices, shards(): all_rows.append(lax.ppermute(all_rows[-1], 'col', perm=pages))  20.2 us
    all_to_all x1, starting transfers between devices, shards(): lax.all_to_all(out_ids, 'row', split_axis=0, concat_axis=0, tiled=True)  14 us
    dot_general x1, matrix products, shards(): lax.dot_general(row_block, lax.all_gather(scored, 'row', axis=1, tiled=Tr...  13.6 us
    all_to_all x1, starting transfers between devices, shards(): lax.all_to_all(outgoing, 'row', split_axis=0, concat_axis=0, tiled=True)  9.11 us
    reshape x1, local copies, waits for them, and re-layouts, shards(): tile_grid.reshape(row_count, TILE, col_count, TILE).transpose(0, 2, 1, 3)  9.11 us
  transfers between devices with their start and end apart: 18, of which 8 were waited for; matrix products, arithmetic and copies ran while one was open for 25% of the time, Pallas kernels for 0%

profile of v1, /device:TPU:65, one launch (start us, length us, event | category | flops | bytes accessed | tf_op | source)
XLA Modules:
  0.0 287.0 jit_solution(9035037917380059363)
XLA Ops:
  7.3 1.2 reduce_sum.60
  8.4 1.1 multiply_reduce_fusion
  9.6 1.1 multiply_convert_fusion.1
  10.6 6.6 %collective-permute-start = (bf16[800,128]{1,0:T(8,128)(2,1)S(1)}, bf16[800,128]{1,0:T(8,128)(2,1)S(1)}, u32[]{:S(2)}, u32[]{:S(2)}) collective-permute-start(bf16[800,128]{1,0:T(8,128)(2,1)S(1)} %multiply_convert_fusion.1), channel_id=1, source_target_pairs={{0,1},{1,2},{2,3},{3,4},{4,5},{5,6},{6,7},{7,8},{8,9},{9,10},{10,1... | collective-permute-start | bytes 614408 | tf_op jit(solution)/shard_map/ppermute | solution.py:35
  17.2 39.9 %collective-permute-start.8 = (bf16[800,128]{1,0:T(8,128)(2,1)S(1)}, bf16[800,128]{1,0:T(8,128)(2,1)S(1)}, u32[]{:S(2)}, u32[]{:S(2)}) collective-permute-start(bf16[800,128]{1,0:T(8,128)(2,1)S(1)} %multiply_convert_fusion.1), channel_id=1, source_target_pairs={{0,15},{1,0},{2,1},{3,2},{4,3},{5,4},{6,5},{7,6},{8,7},{9,8},{10,9... | collective-permute-start | bytes 614408 | tf_op jit(solution)/shard_map/ppermute | solution.py:37
  57.3 0.8 dynamic_slice.7
  58.9 1.9 collective-permute-start.1
  60.9 5.8 %collective-permute-done.1 = bf16[800,128]{1,0:T(8,128)(2,1)S(1)} collective-permute-done((bf16[800,128]{1,0:T(8,128)(2,1)S(1)}, bf16[800,128]{1,0:T(8,128)(2,1)S(1)}, u32[]{:S(2)}, u32[]{:S(2)}) %collective-permute-start.1) | collective-permute-done | bytes 204832 | tf_op jit(solution)/shard_map/ppermute | solution.py:35
  66.6 1.9 collective-permute-start.2
  69.0 4.6 %collective-permute-start.9 = (bf16[800,128]{1,0:T(8,128)(2,1)S(1)}, bf16[800,128]{1,0:T(8,128)(2,1)S(1)}, u32[]{:S(2)}, u32[]{:S(2)}) collective-permute-start(bf16[800,128]{1,0:T(8,128)(2,1)S(1)} %collective-permute-done.8), channel_id=1, source_target_pairs={{0,15},{1,0},{2,1},{3,2},{4,3},{5,4},{6,5},{7,6},{8,7},{9,8},{10,9... | collective-permute-start | bytes 614408 | tf_op jit(solution)/shard_map/ppermute | solution.py:37
  73.6 1.1 collective-permute-done.2
  74.8 1.9 collective-permute-start.3
  77.0 4.8 %collective-permute-start.10 = (bf16[800,128]{1,0:T(8,128)(2,1)S(1)}, bf16[800,128]{1,0:T(8,128)(2,1)S(1)}, u32[]{:S(2)}, u32[]{:S(2)}) collective-permute-start(bf16[800,128]{1,0:T(8,128)(2,1)S(1)} %collective-permute-done.9), channel_id=1, source_target_pairs={{0,15},{1,0},{2,1},{3,2},{4,3},{5,4},{6,5},{7,6},{8,7},{9,8},{10,9... | collective-permute-start | bytes 614408 | tf_op jit(solution)/shard_map/ppermute | solution.py:37
  81.8 1.1 collective-permute-done.3
  82.9 1.9 collective-permute-start.4
  84.9 5.0 %collective-permute-start.11 = (bf16[800,128]{1,0:T(8,128)(2,1)S(1)}, bf16[800,128]{1,0:T(8,128)(2,1)S(1)}, u32[]{:S(2)}, u32[]{:S(2)}) collective-permute-start(bf16[800,128]{1,0:T(8,128)(2,1)S(1)} %collective-permute-done.10), channel_id=1, source_target_pairs={{0,15},{1,0},{2,1},{3,2},{4,3},{5,4},{6,5},{7,6},{8,7},{9,8},{10,9... | collective-permute-start | bytes 614408 | tf_op jit(solution)/shard_map/ppermute | solution.py:37
  89.9 0.7 collective-permute-done.4
  90.6 1.9 collective-permute-start.5
  93.3 14.0 %all-to-all-start = ((s32[16,1,6]{2,1,0:T(1,128)}), s32[16,1,6]{2,1,0:T(1,128)S(1)}, u32[]{:S(2)}, u32[]{:S(2)}) async-start(s32[16,1,6]{2,1,0:T(1,128)} %copy.18), calls=%async_computation | async-start | bytes 16384 | tf_op jit(solution)/shard_map/all_to_all | solution.py:83
  107.3 4.9 %collective-permute-start.12 = (bf16[800,128]{1,0:T(8,128)(2,1)S(1)}, bf16[800,128]{1,0:T(8,128)(2,1)S(1)}, u32[]{:S(2)}, u32[]{:S(2)}) collective-permute-start(bf16[800,128]{1,0:T(8,128)(2,1)S(1)} %collective-permute-done.11), channel_id=1, source_target_pairs={{0,15},{1,0},{2,1},{3,2},{4,3},{5,4},{6,5},{7,6},{8,7},{9,8},{10,9... | collective-permute-start | bytes 614408 | tf_op jit(solution)/shard_map/ppermute | solution.py:37
  112.2 2.0 collective-permute-start.6
  114.3 1.9 collective-permute-done.12
  116.3 5.3 %collective-permute-start.13 = (bf16[800,128]{1,0:T(8,128)(2,1)S(1)}, bf16[800,128]{1,0:T(8,128)(2,1)S(1)}, u32[]{:S(2)}, u32[]{:S(2)}) collective-permute-start(bf16[800,128]{1,0:T(8,128)(2,1)S(1)} %collective-permute-done.12), channel_id=1, source_target_pairs={{0,15},{1,0},{2,1},{3,2},{4,3},{5,4},{6,5},{7,6},{8,7},{9,8},{10,9... | collective-permute-start | bytes 614408 | tf_op jit(solution)/shard_map/ppermute | solution.py:37
  121.6 2.0 collective-permute-start.7
  123.6 1.2 collective-permute-done.13
  124.8 5.5 %collective-permute-start.14 = (bf16[800,128]{1,0:T(8,128)(2,1)S(1)}, bf16[800,128]{1,0:T(8,128)(2,1)S(1)}, u32[]{:S(2)}, u32[]{:S(2)}) collective-permute-start(bf16[800,128]{1,0:T(8,128)(2,1)S(1)} %collective-permute-done.13), channel_id=1, source_target_pairs={{0,15},{1,0},{2,1},{3,2},{4,3},{5,4},{6,5},{7,6},{8,7},{9,8},{10,9... | collective-permute-start | bytes 614408 | tf_op jit(solution)/shard_map/ppermute | solution.py:37
  132.5 0.7 constant_dynamic-update-slice_fusion.28
  136.1 1.8 constant_dynamic-update-slice_fusion.23
  138.6 0.7 constant_dynamic-update-slice_fusion.21
  142.2 0.8 constant_dynamic-update-slice_fusion.16
  144.4 0.7 constant_dynamic-update-slice_fusion.13
  145.1 0.7 constant_dynamic-update-slice_fusion.12
  145.9 0.7 constant_dynamic-update-slice_fusion.11
  146.6 0.8 constant_dynamic-update-slice_fusion.10
  148.8 0.8 constant_dynamic-update-slice_fusion.7
  151.0 0.7 constant_dynamic-update-slice_fusion.4
  151.8 0.7 constant_dynamic-update-slice_fusion.3
  154.6 13.6 %fusion = bf16[256,8,16,128]{3,1,2,0:T(8,128)(2,1)} fusion(bf16[800,2048]{1,0:T(8,128)(2,1)} %all-gather.2.cloned.1.call-done, bf16[800,4096]{1,0:T(8,128)(2,1)} %constant_dynamic-update-slice_fusion, s32[]{:T(128)S(6)} %select_n.171), kind=kOutput, calls=%fused_computation.6 | convolution fusion | flops 6719275008 | bytes 14942212 | tf_op jit(solution)/shard_map/dot_general | solution.py:43
  168.2 9.7 %copy.22 = bf16[256,8,16,128]{3,2,1,0:T(8,128)(2,1)} copy(bf16[256,8,16,128]{3,1,2,0:T(8,128)(2,1)} %fusion) | data formatting | bytes 16777216
  178.0 9.1 %copy.24 = bf16[16,128,16,128]{3,1,2,0:T(8,128)(2,1)} copy(bf16[16,128,16,128]{3,2,1,0:T(8,128)(2,1)} %bitcast.35) | data formatting | bytes 16777216 | tf_op jit(solution)/shard_map/reshape | solution.py:51
  187.1 4.9 %gather_fusion.1 = bf16[96,128,128]{2,1,0:T(8,128)(2,1)S(1)} fusion(bf16[16,16,128,128]{3,2,1,0:T(8,128)(2,1)} %bitcast.36, s32[96]{0:T(128)S(1)} %reshape.311), kind=kCustom, calls=%fused_computation.1 | custom fusion | bytes 6292224 | tf_op jit(solution)/shard_map/gather | solution.py:78
  192.0 1.9 broadcast_select_fusion
  193.9 9.1 %all-to-all-start.1 = ((bf16[16,6,128,128]{3,2,1,0:T(8,128)(2,1)}), bf16[16,6,128,128]{3,2,1,0:T(8,128)(2,1)S(1)}, u32[]{:S(2)}, u32[]{:S(2)}) async-start(bf16[16,6,128,128]{3,2,1,0:T(8,128)(2,1)} %broadcast_select_fusion), calls=%async_computation.1 | async-start | bytes 6291456 | tf_op jit(solution)/shard_map/all_to_all | solution.py:82
  205.5 1.2 gather_fusion.3
  207.4 1.2 compare_select_fusion.6
  208.7 65.3 %all-to-all-done.1 = bf16[16,6,128,128]{3,2,1,0:T(8,128)(2,1)S(1)} async-done(((bf16[16,6,128,128]{3,2,1,0:T(8,128)(2,1)}), bf16[16,6,128,128]{3,2,1,0:T(8,128)(2,1)S(1)}, u32[]{:S(2)}, u32[]{:S(2)}) %all-to-all-start.1) | async-done | bytes 3145760 | tf_op jit(solution)/shard_map/all_to_all | solution.py:82
  274.0 2.7 gather_fusion.2
  276.7 3.4 %fusion.2 = bf16[1,1,96,128,128]{4,3,2,1,0:T(8,128)(2,1)} fusion(bf16[96,128,128]{2,1,0:T(8,128)(2,1)} %gather_fusion.2, pred[96]{0:T(512)(128)(4,1)S(1)} %get-tuple-element.8, pred[96]{0:T(512)(128)(4,1)S(1)} %get-tuple-element.9), kind=kLoop, calls=%fused_computation.9 | loop fusion | flops 3145728 | bytes 6291648 | tf_op jit(solution)/shard_map/jit(_where)/select_n | solution.py:19
  (73 shorter events, 20.8 us)
Async XLA Ops:
  7.2 51.0 %copy-start = (s32[16,16]{1,0:T(8,128)S(1)}, s32[16,16]{1,0:T(8,128)}, u32[]{:S(2)}) copy-start(s32[16,16]{1,0:T(8,128)} %param.4) | copy-start | bytes 3076
  7.2 141.6 %copy-start.1 = (f32[800,128]{1,0:T(8,128)S(1)}, f32[800,128]{1,0:T(8,128)}, u32[]{:S(2)}) copy-start(f32[800,128]{1,0:T(8,128)} %param.3) | copy-start | bytes 1228804
  7.2 147.4 %all-gather.2.cloned.1.call-start = ((), (), s32[]{:S(2)}) async-start(), calls=%async_computation.2 | async-start | bytes 3481600 | tf_op jit(solution)/shard_map/all_gather | solution.py:45
  10.6 46.5 %copy-start.2 = (bf16[800,128]{1,0:T(8,128)(2,1)}, bf16[800,128]{1,0:T(8,128)(2,1)S(1)}, u32[]{:S(2)}) copy-start(bf16[800,128]{1,0:T(8,128)(2,1)S(1)} %multiply_convert_fusion.1) | copy-start | bytes 614404
  10.6 48.3 %collective-permute-start = (bf16[800,128]{1,0:T(8,128)(2,1)S(1)}, bf16[800,128]{1,0:T(8,128)(2,1)S(1)}, u32[]{:S(2)}, u32[]{:S(2)}) collective-permute-start(bf16[800,128]{1,0:T(8,128)(2,1)S(1)} %multiply_convert_fusion.1), channel_id=1, source_target_pairs={{0,1},{1,2},{2,3},{3,4},{4,5},{5,6},{6,7},{7,8},{8,9},{9,10},{10,1... | collective-permute-start | bytes 614408 | tf_op jit(solution)/shard_map/ppermute | solution.py:35
  17.2 51.8 %collective-permute-start.8 = (bf16[800,128]{1,0:T(8,128)(2,1)S(1)}, bf16[800,128]{1,0:T(8,128)(2,1)S(1)}, u32[]{:S(2)}, u32[]{:S(2)}) collective-permute-start(bf16[800,128]{1,0:T(8,128)(2,1)S(1)} %multiply_convert_fusion.1), channel_id=1, source_target_pairs={{0,15},{1,0},{2,1},{3,2},{4,3},{5,4},{6,5},{7,6},{8,7},{9,8},{10,9... | collective-permute-start | bytes 614408 | tf_op jit(solution)/shard_map/ppermute | solution.py:37
  58.9 7.7 %collective-permute-start.1 = (bf16[800,128]{1,0:T(8,128)(2,1)S(1)}, bf16[800,128]{1,0:T(8,128)(2,1)S(1)}, u32[]{:S(2)}, u32[]{:S(2)}) collective-permute-start(bf16[800,128]{1,0:T(8,128)(2,1)S(1)} %collective-permute-done), channel_id=1, source_target_pairs={{0,1},{1,2},{2,3},{3,4},{4,5},{5,6},{6,7},{7,8},{8,9},{9,10},{10,1... | collective-permute-start | bytes 614408 | tf_op jit(solution)/shard_map/ppermute | solution.py:35
  66.6 8.1 %collective-permute-start.2 = (bf16[800,128]{1,0:T(8,128)(2,1)S(1)}, bf16[800,128]{1,0:T(8,128)(2,1)S(1)}, u32[]{:S(2)}, u32[]{:S(2)}) collective-permute-start(bf16[800,128]{1,0:T(8,128)(2,1)S(1)} %collective-permute-done.1), channel_id=1, source_target_pairs={{0,1},{1,2},{2,3},{3,4},{4,5},{5,6},{6,7},{7,8},{8,9},{9,10},{10,1... | collective-permute-start | bytes 614408 | tf_op jit(solution)/shard_map/ppermute | solution.py:35
  69.0 8.0 %collective-permute-start.9 = (bf16[800,128]{1,0:T(8,128)(2,1)S(1)}, bf16[800,128]{1,0:T(8,128)(2,1)S(1)}, u32[]{:S(2)}, u32[]{:S(2)}) collective-permute-start(bf16[800,128]{1,0:T(8,128)(2,1)S(1)} %collective-permute-done.8), channel_id=1, source_target_pairs={{0,15},{1,0},{2,1},{3,2},{4,3},{5,4},{6,5},{7,6},{8,7},{9,8},{10,9... | collective-permute-start | bytes 614408 | tf_op jit(solution)/shard_map/ppermute | solution.py:37
  74.8 8.1 %collective-permute-start.3 = (bf16[800,128]{1,0:T(8,128)(2,1)S(1)}, bf16[800,128]{1,0:T(8,128)(2,1)S(1)}, u32[]{:S(2)}, u32[]{:S(2)}) collective-permute-start(bf16[800,128]{1,0:T(8,128)(2,1)S(1)} %collective-permute-done.2), channel_id=1, source_target_pairs={{0,1},{1,2},{2,3},{3,4},{4,5},{5,6},{6,7},{7,8},{8,9},{9,10},{10,1... | collective-permute-start | bytes 614408 | tf_op jit(solution)/shard_map/ppermute | solution.py:35
  77.0 7.9 %collective-permute-start.10 = (bf16[800,128]{1,0:T(8,128)(2,1)S(1)}, bf16[800,128]{1,0:T(8,128)(2,1)S(1)}, u32[]{:S(2)}, u32[]{:S(2)}) collective-permute-start(bf16[800,128]{1,0:T(8,128)(2,1)S(1)} %collective-permute-done.9), channel_id=1, source_target_pairs={{0,15},{1,0},{2,1},{3,2},{4,3},{5,4},{6,5},{7,6},{8,7},{9,8},{10,9... | collective-permute-start | bytes 614408 | tf_op jit(solution)/shard_map/ppermute | solution.py:37
  82.9 7.7 %collective-permute-start.4 = (bf16[800,128]{1,0:T(8,128)(2,1)S(1)}, bf16[800,128]{1,0:T(8,128)(2,1)S(1)}, u32[]{:S(2)}, u32[]{:S(2)}) collective-permute-start(bf16[800,128]{1,0:T(8,128)(2,1)S(1)} %collective-permute-done.3), channel_id=1, source_target_pairs={{0,1},{1,2},{2,3},{3,4},{4,5},{5,6},{6,7},{7,8},{8,9},{9,10},{10,1... | collective-permute-start | bytes 614408 | tf_op jit(solution)/shard_map/ppermute | solution.py:35
  84.9 22.4 %collective-permute-start.11 = (bf16[800,128]{1,0:T(8,128)(2,1)S(1)}, bf16[800,128]{1,0:T(8,128)(2,1)S(1)}, u32[]{:S(2)}, u32[]{:S(2)}) collective-permute-start(bf16[800,128]{1,0:T(8,128)(2,1)S(1)} %collective-permute-done.10), channel_id=1, source_target_pairs={{0,15},{1,0},{2,1},{3,2},{4,3},{5,4},{6,5},{7,6},{8,7},{9,8},{10,9... | collective-permute-start | bytes 614408 | tf_op jit(solution)/shard_map/ppermute | solution.py:37
  90.6 21.5 %collective-permute-start.5 = (bf16[800,128]{1,0:T(8,128)(2,1)S(1)}, bf16[800,128]{1,0:T(8,128)(2,1)S(1)}, u32[]{:S(2)}, u32[]{:S(2)}) collective-permute-start(bf16[800,128]{1,0:T(8,128)(2,1)S(1)} %collective-permute-done.4), channel_id=1, source_target_pairs={{0,1},{1,2},{2,3},{3,4},{4,5},{5,6},{6,7},{7,8},{8,9},{9,10},{10,1... | collective-permute-start | bytes 614408 | tf_op jit(solution)/shard_map/ppermute | solution.py:35
  93.3 100.7 %all-to-all-start = ((s32[16,1,6]{2,1,0:T(1,128)}), s32[16,1,6]{2,1,0:T(1,128)S(1)}, u32[]{:S(2)}, u32[]{:S(2)}) async-start(s32[16,1,6]{2,1,0:T(1,128)} %copy.18), calls=%async_computation | async-start | bytes 16384 | tf_op jit(solution)/shard_map/all_to_all | solution.py:83
  107.3 9.0 %collective-permute-start.12 = (bf16[800,128]{1,0:T(8,128)(2,1)S(1)}, bf16[800,128]{1,0:T(8,128)(2,1)S(1)}, u32[]{:S(2)}, u32[]{:S(2)}) collective-permute-start(bf16[800,128]{1,0:T(8,128)(2,1)S(1)} %collective-permute-done.11), channel_id=1, source_target_pairs={{0,15},{1,0},{2,1},{3,2},{4,3},{5,4},{6,5},{7,6},{8,7},{9,8},{10,9... | collective-permute-start | bytes 614408 | tf_op jit(solution)/shard_map/ppermute | solution.py:37
  112.2 9.4 %collective-permute-start.6 = (bf16[800,128]{1,0:T(8,128)(2,1)S(1)}, bf16[800,128]{1,0:T(8,128)(2,1)S(1)}, u32[]{:S(2)}, u32[]{:S(2)}) collective-permute-start(bf16[800,128]{1,0:T(8,128)(2,1)S(1)} %collective-permute-done.5), channel_id=1, source_target_pairs={{0,1},{1,2},{2,3},{3,4},{4,5},{5,6},{6,7},{7,8},{8,9},{9,10},{10,1... | collective-permute-start | bytes 614408 | tf_op jit(solution)/shard_map/ppermute | solution.py:35
  116.3 8.6 %collective-permute-start.13 = (bf16[800,128]{1,0:T(8,128)(2,1)S(1)}, bf16[800,128]{1,0:T(8,128)(2,1)S(1)}, u32[]{:S(2)}, u32[]{:S(2)}) collective-permute-start(bf16[800,128]{1,0:T(8,128)(2,1)S(1)} %collective-permute-done.12), channel_id=1, source_target_pairs={{0,15},{1,0},{2,1},{3,2},{4,3},{5,4},{6,5},{7,6},{8,7},{9,8},{10,9... | collective-permute-start | bytes 614408 | tf_op jit(solution)/shard_map/ppermute | solution.py:37
  121.6 8.7 %collective-permute-start.7 = (bf16[800,128]{1,0:T(8,128)(2,1)S(1)}, bf16[800,128]{1,0:T(8,128)(2,1)S(1)}, u32[]{:S(2)}, u32[]{:S(2)}) collective-permute-start(bf16[800,128]{1,0:T(8,128)(2,1)S(1)} %collective-permute-done.6), channel_id=1, source_target_pairs={{0,1},{1,2},{2,3},{3,4},{4,5},{5,6},{6,7},{7,8},{8,9},{9,10},{10,1... | collective-permute-start | bytes 614408 | tf_op jit(solution)/shard_map/ppermute | solution.py:35
  124.8 17.4 %collective-permute-start.14 = (bf16[800,128]{1,0:T(8,128)(2,1)S(1)}, bf16[800,128]{1,0:T(8,128)(2,1)S(1)}, u32[]{:S(2)}, u32[]{:S(2)}) collective-permute-start(bf16[800,128]{1,0:T(8,128)(2,1)S(1)} %collective-permute-done.13), channel_id=1, source_target_pairs={{0,15},{1,0},{2,1},{3,2},{4,3},{5,4},{6,5},{7,6},{8,7},{9,8},{10,9... | collective-permute-start | bytes 614408 | tf_op jit(solution)/shard_map/ppermute | solution.py:37
  193.9 80.0 %all-to-all-start.1 = ((bf16[16,6,128,128]{3,2,1,0:T(8,128)(2,1)}), bf16[16,6,128,128]{3,2,1,0:T(8,128)(2,1)S(1)}, u32[]{:S(2)}, u32[]{:S(2)}) async-start(bf16[16,6,128,128]{3,2,1,0:T(8,128)(2,1)} %broadcast_select_fusion), calls=%async_computation.1 | async-start | bytes 6291456 | tf_op jit(solution)/shard_map/all_to_all | solution.py:82
Sparse Core Ops, SparseCore 0:
  57.4 46.6 all-gather.1
